TPU v7x, 32 devices: a whole 2x2x4 slice. The times are simulated.
32 devices in a mesh: dp: 8 (over z, y), mp: 4 (over x, core).
Axes of the slice: x: 2, y: 2, z: 4, core: 2. Of those that a mesh axis runs over, the one named last changes fastest.
Arguments:
- tokens: bfloat16 [8192, 4096], P('dp', 'mp'), may hold values from -6 to 6
- right_weight: bfloat16 [64, 64, 64], P('mp', 'dp'), may hold values from -0.75 to 0.75
- left_weight: bfloat16 [64, 64, 64], P('mp', 'dp'), may hold values from -0.75 to 0.75
- cotangent: bfloat16 [8192, 4096], P('dp', 'mp'), may hold values from -0.06591797 to 0.06591797
Outputs:
- activated: bfloat16 [8192, 4096], P('dp', 'mp')
- grad_right: float32 [64, 64, 64], P('mp', 'dp')
- grad_left: float32 [64, 64, 64], P('mp', 'dp')
All inputs are finite; a program needn't handle non-finite values.
Results may differ from a plain program's by a relative error of at most 0.0056.
Values may be sent and summed in bfloat16 or wider, within the bound.
A program may use at most 64 MiB of HBM per device.

v0:
```python
import functools

import jax
import jax.numpy as jnp
from jax import lax
from jax.experimental import pallas as pl
from jax.experimental.pallas import tpu as pltpu
from jax.sharding import PartitionSpec as P

MESH = pl.DeviceIdType.MESH
BF = jnp.bfloat16
F32 = jnp.float32
CHUNKS = 8


def iota(shape, dim):
    line = tuple(n if axis == dim else 1 for axis, n in enumerate(shape))
    return lax.broadcasted_iota(jnp.int32, line, dim)


def ones_where(cond):
    return jnp.where(cond, 1.0, 0.0).astype(BF)


def dot_nn(a, b):
    return lax.dot_general(a, b, (((1,), (0,)), ((), ())), preferred_element_type=F32)


def dot_nt(a, b):
    return lax.dot_general(a, b, (((1,), (1,)), ((), ())), preferred_element_type=F32)


def dot_tn(a, b):
    return lax.dot_general(a, b, (((0,), (0,)), ((), ())), preferred_element_type=F32)


def join(parts, axis=1):
    return parts[0] if len(parts) == 1 else jnp.concatenate(parts, axis=axis)


class Sizes:
    def __init__(self, n_dp, n_mp, tok_rows, features, width):
        self.dp, self.mp = n_dp, n_mp
        self.tok, self.feat, self.bs = tok_rows, features, width
        self.own = features // width
        self.blocks = self.own * n_mp
        self.rows = width // n_dp
        self.orow = self.own * self.rows
        self.pad = max(self.own, 16)
        self.gs = max(1, 128 // (self.own * self.own))
        self.groups = n_mp // self.gs
        self.ng = self.gs * self.own * self.own
        self.kg = self.gs * features
        self.jg = self.ng // 128
        self.jl = self.own // self.jg
        self.nj = self.ng // self.jg
        self.rh = self.groups * self.nj
        self.fj = self.jl * width
        self.n = n_dp * n_mp
        self.direct = self.pad == self.own and self.orow % 128 == 0
        self.tc = tok_rows // CHUNKS


def kernel(z, x_hbm, cot_hbm, rw_hbm, lw_hbm, act, gr_ref, gl_ref,
           xfull, cot, rw_v, lw_v, rwt, lwt, rg, lg, p1, p2, wt, lt, gracc, glacc,
           rsend, rrecv, lsend, lrecv,
           x_recv, x_send, x_local, c_local, w_local,
           rw_send, rw_recv, lw_send, lw_recv, gr_send, gr_recv, gl_send, gl_recv):
    d, p = lax.axis_index("dp"), lax.axis_index("mp")
    me = d * z.mp + p
    core = lax.rem(p, 2)
    partner = p + 1 - 2 * core
    chip = p // 2
    chips = z.mp // 2

    barrier = pltpu.get_barrier_semaphore()

    @pl.loop(1, z.n)
    def _(s):
        o = lax.rem(me + s, z.n)
        pl.semaphore_signal(barrier, inc=1, device_id=(o // z.mp, lax.rem(o, z.mp)), device_id_type=MESH)

    def rows(c):
        return pl.ds(pl.multiple_of(c * z.tc, z.tc), z.tc)

    def local_x(c):
        return pltpu.make_async_copy(x_hbm.at[rows(c)], xfull.at[p, rows(c)], x_local.at[c])

    def local_c(c):
        return pltpu.make_async_copy(cot_hbm.at[rows(c)], cot.at[rows(c)], c_local.at[c])

    def send_own(c, kind, target):
        return pltpu.make_async_remote_copy(
            src_ref=x_hbm.at[rows(c)], dst_ref=xfull.at[p, rows(c)],
            send_sem=x_send.at[kind, c], recv_sem=x_recv.at[p, c],
            device_id=(d, target), device_id_type=MESH)

    def forward(c, kind, source):
        return pltpu.make_async_remote_copy(
            src_ref=xfull.at[source, rows(c)], dst_ref=xfull.at[source, rows(c)],
            send_sem=x_send.at[kind, c], recv_sem=x_recv.at[source, c],
            device_id=(d, partner), device_id_type=MESH)

    def arrived(c, source):
        pltpu.make_async_remote_copy(
            src_ref=xfull.at[source, rows(c)], dst_ref=xfull.at[source, rows(c)],
            send_sem=x_send.at[0, c], recv_sem=x_recv.at[source, c],
            device_id=(d, partner), device_id_type=MESH).wait_recv()

    def same_core(s):
        return lax.rem(chip + s, chips) * 2 + core

    def other_core(s):
        return lax.rem(chip + s, chips) * 2 + 1 - core

    @pl.loop(0, CHUNKS)
    def _(c):
        local_x(c).start()
        local_c(c).start()

    local_r = pltpu.make_async_copy(rw_hbm, rw_v, w_local.at[0])
    local_r.start()
    local_l = pltpu.make_async_copy(lw_hbm, lw_v, w_local.at[1])
    local_l.start()
    local_r.wait()
    local_l.wait()
    shape = (z.mp * z.pad, z.bs)
    a, b = iota(shape, 0), iota(shape, 1)
    wide = ones_where((a % z.pad < z.own) & (b == (a // z.pad) * z.own + a % z.pad))
    rwt[...] = dot_nt(wide, rw_v[...]).astype(BF).reshape(z.mp, z.pad, z.orow)
    shape = (z.bs, z.bs)
    lwt[...] = dot_nt(ones_where(iota(shape, 0) == iota(shape, 1)), lw_v[...]).astype(BF)
    rg[me] = rwt[p]
    lg[d] = lwt[...]

    pl.semaphore_wait(barrier, z.n - 1)

    def send_x(c):
        for s in range(1, chips):
            send_own(c, s, same_core(s)).start()
        send_own(c, 0, partner).start()

    send_x(0)

    @pl.loop(1, z.n)
    def _(s):
        o = lax.rem(me + s, z.n)
        q = lax.rem(o, z.mp)
        pltpu.make_async_remote_copy(
            src_ref=rwt.at[q], dst_ref=rg.at[me], send_sem=rw_send, recv_sem=rw_recv,
            device_id=(o // z.mp, q), device_id_type=MESH).start()

    @pl.loop(1, z.dp)
    def _(s):
        pltpu.make_async_remote_copy(
            src_ref=lwt, dst_ref=lg.at[d], send_sem=lw_send, recv_sem=lw_recv,
            device_id=(lax.rem(d + s, z.dp), p), device_id_type=MESH).start()

    @pl.loop(1, CHUNKS)
    def _(c):
        send_x(c)

    for dd in range(z.dp):
        shape = (z.orow, z.feat)
        a, b = iota(shape, 0), iota(shape, 1)
        source = (b // z.bs) * z.rows + (b % z.bs) - dd * z.rows
        inside = (b % z.bs) // z.rows == dd
        p1[dd] = ones_where(inside & (a == source))
        shape = (z.orow, z.blocks * z.own)
        a, b = iota(shape, 0), iota(shape, 1)
        jg = b // z.rh
        i_all = (b % z.rh) // z.jl
        j = jg * z.jl + b % z.jl
        inside = i_all // z.rows == dd
        p2[dd] = ones_where(inside & (a == j * z.rows + i_all % z.rows))
    gracc[...] = jnp.zeros_like(gracc)
    glacc[...] = jnp.zeros_like(glacc)

    def count(ref, sem):
        pltpu.make_async_copy(ref, ref, sem).wait()

    count(lg.at[pl.ds(0, z.dp - 1)], lw_recv)
    left = None
    for dd in range(z.dp):
        part = dot_nn(lg[dd], p2[dd])
        left = part if left is None else left + part
    left = left.astype(BF)
    shape = (z.fj, z.bs)
    spread = ones_where(iota(shape, 0) % z.bs == iota(shape, 1))
    for jg in range(z.jg):
        piece = dot_nn(spread, left[:, jg * z.rh:(jg + 1) * z.rh])
        keep = iota((z.fj, z.rh), 0) // z.bs == iota((z.fj, z.rh), 1) % z.jl
        lt[jg] = jnp.where(keep, piece, 0.0).astype(BF)

    count(rg.at[pl.ds(0, z.n - 1)], rw_recv)
    right = None
    for dd in range(z.dp):
        part = dot_nn(rg[dd * z.mp:(dd + 1) * z.mp].reshape(z.mp * z.pad, z.orow), p1[dd])
        right = part if right is None else right + part
    right = right.astype(BF)
    for g in range(z.groups):
        for s in range(z.gs):
            shape = (z.ng, z.mp * z.pad)
            a, b = iota(shape, 0), iota(shape, 1)
            j = (a // z.nj) * z.jl + a % z.jl
            src = (a % z.nj) // (z.own * z.jl)
            pick = ones_where((src == s) & (b == (g * z.gs + s) * z.pad + j))
            piece = dot_nn(pick, right)
            shape = (z.ng, z.feat)
            keep = (iota(shape, 0) // z.jl) % z.own == iota(shape, 1) // z.bs
            wt[g, :, s * z.feat:(s + 1) * z.feat] = jnp.where(keep, piece, 0.0).astype(BF)

    @pl.loop(0, CHUNKS)
    def _(c):
        local_x(c).wait()
        local_c(c).wait()
        for s in range(1, chips):
            arrived(c, same_core(s))
            forward(c, chips + s, same_core(s)).start()
        arrived(c, partner)
        for s in range(1, chips):
            arrived(c, other_core(s))
        r = rows(c)
        xs = [join([xfull[g * z.gs + s, r] for s in range(z.gs)]) for g in range(z.groups)]
        inner = [dot_nt(xs[g], wt[g]).astype(BF) for g in range(z.groups)]
        back = []
        for jg in range(z.jg):
            mixed = join([v[:, jg * z.nj:(jg + 1) * z.nj] for v in inner])
            pre = dot_nt(mixed, lt[jg])
            cdf = 0.5 * (1.0 + lax.erf(pre * 0.7071067811865476))
            slope = cdf + pre * (jnp.exp(-0.5 * pre * pre) * 0.3989422804014327)
            cols = pl.ds(jg * z.fj, z.fj)
            act[r, cols] = (pre * cdf).astype(BF)
            dpre = (cot[r, cols].astype(F32) * slope).astype(BF)
            glacc[jg] += dot_tn(dpre, mixed)
            back.append(dot_nn(dpre, lt[jg]).astype(BF))
        for g in range(z.groups):
            dinner = join([v[:, g * z.nj:(g + 1) * z.nj] for v in back])
            gracc[g] += dot_tn(dinner, xs[g])

    shape = (z.bs, z.fj)
    fold = ones_where(iota(shape, 1) % z.bs == iota(shape, 0))
    lefts = []
    for jg in range(z.jg):
        keep = iota((z.fj, z.rh), 0) // z.bs == iota((z.fj, z.rh), 1) % z.jl
        lefts.append(dot_nn(fold, jnp.where(keep, glacc[jg], 0.0).astype(BF)).astype(BF))
    left = join(lefts)
    for dd in range(z.dp):
        lsend[dd] = dot_nt(left, p2[dd]).astype(BF)

    @pl.loop(1, z.dp)
    def _(s):
        o = lax.rem(d + s, z.dp)
        pltpu.make_async_remote_copy(
            src_ref=lsend.at[o], dst_ref=lrecv.at[d], send_sem=gl_send, recv_sem=gl_recv,
            device_id=(o, p), device_id_type=MESH).start()

    pieces = []
    for g in range(z.groups):
        for s in range(z.gs):
            shape = (z.pad, z.ng)
            a, b = iota(shape, 0), iota(shape, 1)
            j = (b // z.nj) * z.jl + b % z.jl
            src = (b % z.nj) // (z.own * z.jl)
            pick = ones_where((src == s) & (a == j))
            shape = (z.ng, z.feat)
            keep = (iota(shape, 0) // z.jl) % z.own == iota(shape, 1) // z.bs
            piece = jnp.where(keep, gracc[g, :, s * z.feat:(s + 1) * z.feat], 0.0).astype(BF)
            pieces.append(dot_nn(pick, piece).astype(BF))
    pieces = join(pieces, axis=0)
    for dd in range(z.dp):
        owned = dot_nt(pieces, p1[dd]).astype(BF)
        rsend[dd * z.mp:(dd + 1) * z.mp] = owned.reshape(z.mp, z.pad, z.orow)

    @pl.loop(1, z.n)
    def _(s):
        o = lax.rem(me + s, z.n)
        pltpu.make_async_remote_copy(
            src_ref=rsend.at[o], dst_ref=rrecv.at[me], send_sem=gr_send, recv_sem=gr_recv,
            device_id=(o // z.mp, lax.rem(o, z.mp)), device_id_type=MESH).start()

    lrecv[d] = lsend[d]
    rrecv[me] = rsend[me]

    @pl.loop(0, CHUNKS)
    def _(c):
        for s in range(1, chips):
            send_own(c, s, same_core(s)).wait_send()
            forward(c, chips + s, same_core(s)).wait_send()
        send_own(c, 0, partner).wait_send()

    count(rg.at[pl.ds(0, z.n - 1)], rw_send)
    count(lg.at[pl.ds(0, z.dp - 1)], lw_send)

    count(lrecv.at[pl.ds(0, z.dp - 1)], gl_recv)
    total = lrecv[0].astype(F32)
    for dd in range(1, z.dp):
        total = total + lrecv[dd].astype(F32)
    gl_ref[...] = total.T if z.direct else total
    count(rrecv.at[pl.ds(0, z.n - 1)], gr_recv)
    total = rrecv[0:z.mp].astype(F32)
    for dd in range(1, z.dp):
        total = total + rrecv[dd * z.mp:(dd + 1) * z.mp].astype(F32)
    gr_ref[...] = total.reshape(z.blocks, z.orow).T if z.direct else total
    count(lsend.at[pl.ds(0, z.dp - 1)], gl_send)
    count(rsend.at[pl.ds(0, z.n - 1)], gr_send)


def shards(z, tokens, right_weight, left_weight, cotangent):
    rw = right_weight.reshape(z.orow, z.bs)
    lw = left_weight.reshape(z.orow, z.bs)
    hbm = pl.BlockSpec(memory_space=pltpu.HBM)
    vmem = pl.BlockSpec(memory_space=pltpu.VMEM)
    dma = pltpu.SemaphoreType.DMA
    act, gr, gl = pl.pallas_call(
        functools.partial(kernel, z),
        out_shape=(
            pltpu.VMEM((z.tok, z.feat), BF),
            jax.ShapeDtypeStruct((z.orow, z.bs) if z.direct else (z.mp, z.pad, z.orow), F32),
            jax.ShapeDtypeStruct((z.orow, z.bs) if z.direct else (z.bs, z.orow), F32),
        ),
        in_specs=[hbm] * 4,
        out_specs=(vmem, vmem, vmem),
        scratch_shapes=[
            pltpu.VMEM((z.mp, z.tok, z.feat), BF),
            pltpu.VMEM((z.tok, z.feat), BF),
            pltpu.VMEM((z.orow, z.bs), BF),
            pltpu.VMEM((z.orow, z.bs), BF),
            pltpu.VMEM((z.mp, z.pad, z.orow), BF),
            pltpu.VMEM((z.bs, z.orow), BF),
            pltpu.VMEM((z.n, z.pad, z.orow), BF),
            pltpu.VMEM((z.dp, z.bs, z.orow), BF),
            pltpu.VMEM((z.dp, z.orow, z.feat), BF),
            pltpu.VMEM((z.dp, z.orow, z.blocks * z.own), BF),
            pltpu.VMEM((z.groups, z.ng, z.kg), BF),
            pltpu.VMEM((z.jg, z.fj, z.rh), BF),
            pltpu.VMEM((z.groups, z.ng, z.kg), F32),
            pltpu.VMEM((z.jg, z.fj, z.rh), F32),
            pltpu.VMEM((z.n, z.pad, z.orow), BF),
            pltpu.VMEM((z.n, z.pad, z.orow), BF),
            pltpu.VMEM((z.dp, z.bs, z.orow), BF),
            pltpu.VMEM((z.dp, z.bs, z.orow), BF),
            dma((z.mp, CHUNKS)),
            dma((z.mp, CHUNKS)),
            dma((CHUNKS,)),
            dma((CHUNKS,)),
            dma((2,)),
            dma, dma, dma, dma, dma, dma, dma, dma,
        ],
        compiler_params=pltpu.CompilerParams(
            collective_id=0, has_side_effects=True, vmem_limit_bytes=61 * 1024 * 1024),
    )(tokens, cotangent, rw, lw)
    if z.direct:
        return act, gr.reshape(z.own, z.rows, z.bs), gl.reshape(z.own, z.rows, z.bs)
    gr = gr[:, :z.own].reshape(z.mp * z.own, z.own, z.rows).transpose(1, 2, 0)
    gl = gl.reshape(z.bs, z.own, z.rows).transpose(1, 2, 0)
    return act, gr, gl


def solution(mesh):
    n_dp, n_mp = mesh.shape["dp"], mesh.shape["mp"]

    def step(tokens, right_weight, left_weight, cotangent):
        z = Sizes(n_dp, n_mp, tokens.shape[0] // n_dp, tokens.shape[1] // n_mp, right_weight.shape[1])
        return jax.shard_map(
            functools.partial(shards, z),
            mesh=mesh,
            in_specs=(P("dp", "mp"), P("mp", "dp", None), P("mp", "dp", None), P("dp", "mp")),
            out_specs=(P("dp", "mp"), P("mp", "dp", None), P("mp", "dp", None)),
            check_vma=False,
        )(tokens, right_weight, left_weight, cotangent)

    return step
```

profile of v0, /device:TPU:1, one launch (start us, length us, event | category | flops | bytes accessed | tf_op | source)
XLA Modules:
  0.0 71.8 jit_solution(4714712684108868352)
XLA Ops:
  0.6 68.6 %shard_map.67 = (bf16[1024,1024]{1,0:T(8,128)(2,1)S(1)}, f32[128,64]{1,0:T(8,128)}, f32[128,64]{1,0:T(8,128)}) custom-call(bf16[1024,1024]{1,0:T(8,128)(2,1)} %x_hbm.1, bf16[1024,1024]{1,0:T(8,128)(2,1)} %cot_hbm.1, bf16[128,64]{1,0:T(8,128)(2,1)} %bitcast.6, bf16[128,64]{1,0:T(8,128)(2,1)} %bitcast.7), custom_call_target="tpu_custom_call" | custom-call | tf_op jit(solution)/shard_map/pallas_call | solution.py:315
  69.2 0.0 copy-start.1
  69.2 0.0 copy-start
  69.3 1.3 %copy.10 = bf16[1024,1024]{1,0:T(8,128)(2,1)} copy(bf16[1024,1024]{1,0:T(8,128)(2,1)S(1)} %get-tuple-element.9) | data formatting | bytes 4194304
  70.6 0.0 copy-done.1
  70.6 0.6 copy.11
  71.2 0.0 copy-done
  71.2 0.6 copy.12
Async XLA Ops:
  69.2 1.3 %copy-start.1 = (f32[128,64]{1,0:T(8,128)S(1)}, f32[128,64]{1,0:T(8,128)}, u32[]{:S(2)}) copy-start(f32[128,64]{1,0:T(8,128)} %get-tuple-element.7) | copy-start | bytes 98308
  69.2 2.0 %copy-start = (f32[128,64]{1,0:T(8,128)S(1)}, f32[128,64]{1,0:T(8,128)}, u32[]{:S(2)}) copy-start(f32[128,64]{1,0:T(8,128)} %get-tuple-element.8) | copy-start | bytes 98308
where the time goes:
time: 72.4 us; the launch traced here: 71.8 us
  Pallas kernels  68.6 us (95%)
  local copies, waits for them, and re-layouts  2.59 us (4%)
    pallas_call x1, Pallas kernels, shards(): pl.pallas_call(functools.partial(kernel, z), out_shape=(pltpu.VMEM((z.tok...  68.6 us
    unnamed x7, local copies, waits for them, and re-layouts  2.59 us

commit v1 on v0

--- a/solution.py
+++ b/solution.py
@@ -11,6 +11,7 @@
 BF = jnp.bfloat16
 F32 = jnp.float32
 CHUNKS = 8
+TAIL = (1,)
 
 
 def iota(shape, dim):
@@ -36,6 +37,11 @@
 
 def join(parts, axis=1):
     return parts[0] if len(parts) == 1 else jnp.concatenate(parts, axis=axis)
+
+
+def across(index, r):
+    bit = 1 << r
+    return index + bit - 2 * bit * lax.rem(index // bit, 2)
 
 
 class Sizes:
@@ -59,13 +65,22 @@
         self.n = n_dp * n_mp
         self.direct = self.pad == self.own and self.orow % 128 == 0
         self.tc = tok_rows // CHUNKS
+        self.main = CHUNKS - 1
+        self.tail = []
+        start = self.main * self.tc
+        for part in TAIL:
+            self.tail.append((self.main + len(self.tail), start, self.tc // part))
+            start += self.tc // part
+        self.parts = self.main + len(self.tail)
+        self.rounds = n_dp.bit_length() - 1
+        self.cube = n_dp == 1 << self.rounds
 
 
 def kernel(z, x_hbm, cot_hbm, rw_hbm, lw_hbm, act, gr_ref, gl_ref,
            xfull, cot, rw_v, lw_v, rwt, lwt, rg, lg, p1, p2, wt, lt, gracc, glacc,
            rsend, rrecv, lsend, lrecv,
            x_recv, x_send, x_local, c_local, w_local,
-           rw_send, rw_recv, lw_send, lw_recv, gr_send, gr_recv, gl_send, gl_recv):
+           rw_send, rw_recv, lw_send, lw_recv, gr_send, gr_recv, gl_send, gl_recv, ra_send, ra_recv, met):
     d, p = lax.axis_index("dp"), lax.axis_index("mp")
     me = d * z.mp + p
     core = lax.rem(p, 2)
@@ -73,55 +88,70 @@
     chip = p // 2
     chips = z.mp // 2
 
+    def same_core(s):
+        return lax.rem(chip + s, chips) * 2 + core
+
+    def other_core(s):
+        return lax.rem(chip + s, chips) * 2 + 1 - core
+
     barrier = pltpu.get_barrier_semaphore()
-
-    @pl.loop(1, z.n)
-    def _(s):
-        o = lax.rem(me + s, z.n)
-        pl.semaphore_signal(barrier, inc=1, device_id=(o // z.mp, lax.rem(o, z.mp)), device_id_type=MESH)
-
-    def rows(c):
-        return pl.ds(pl.multiple_of(c * z.tc, z.tc), z.tc)
-
-    def local_x(c):
-        return pltpu.make_async_copy(x_hbm.at[rows(c)], xfull.at[p, rows(c)], x_local.at[c])
-
-    def local_c(c):
-        return pltpu.make_async_copy(cot_hbm.at[rows(c)], cot.at[rows(c)], c_local.at[c])
-
-    def send_own(c, kind, target):
+    if z.cube:
+        for s in range(1, z.mp):
+            pl.semaphore_signal(barrier, inc=1, device_id=(d, lax.rem(p + s, z.mp)), device_id_type=MESH)
+        for r in range(z.rounds):
+            pl.semaphore_signal(barrier, inc=1, device_id=(across(d, r), p), device_id_type=MESH)
+        near = z.mp - 1 + z.rounds
+    else:
+        @pl.loop(1, z.n)
+        def _(s):
+            o = lax.rem(me + s, z.n)
+            pl.semaphore_signal(barrier, inc=1, device_id=(o // z.mp, lax.rem(o, z.mp)), device_id_type=MESH)
+        near = z.n - 1
+
+    def full(c):
+        return c, pl.multiple_of(c * z.tc, z.tc), z.tc
+
+    def local_x(part):
+        c, start, size = part
+        return pltpu.make_async_copy(x_hbm.at[pl.ds(start, size)], xfull.at[p, pl.ds(start, size)], x_local.at[c])
+
+    def local_c(part):
+        c, start, size = part
+        return pltpu.make_async_copy(cot_hbm.at[pl.ds(start, size)], cot.at[pl.ds(start, size)], c_local.at[c])
+
+    def send_own(part, kind, target):
+        c, start, size = part
         return pltpu.make_async_remote_copy(
-            src_ref=x_hbm.at[rows(c)], dst_ref=xfull.at[p, rows(c)],
+            src_ref=x_hbm.at[pl.ds(start, size)], dst_ref=xfull.at[p, pl.ds(start, size)],
             send_sem=x_send.at[kind, c], recv_sem=x_recv.at[p, c],
             device_id=(d, target), device_id_type=MESH)
 
-    def forward(c, kind, source):
+    def forward(part, kind, source):
+        c, start, size = part
         return pltpu.make_async_remote_copy(
-            src_ref=xfull.at[source, rows(c)], dst_ref=xfull.at[source, rows(c)],
+            src_ref=xfull.at[source, pl.ds(start, size)], dst_ref=xfull.at[source, pl.ds(start, size)],
             send_sem=x_send.at[kind, c], recv_sem=x_recv.at[source, c],
             device_id=(d, partner), device_id_type=MESH)
 
-    def arrived(c, source):
-        pltpu.make_async_remote_copy(
-            src_ref=xfull.at[source, rows(c)], dst_ref=xfull.at[source, rows(c)],
+    def arrived(part, source):
+        c, start, size = part
+        pltpu.make_async_remote_copy(
+            src_ref=xfull.at[source, pl.ds(start, size)], dst_ref=xfull.at[source, pl.ds(start, size)],
             send_sem=x_send.at[0, c], recv_sem=x_recv.at[source, c],
             device_id=(d, partner), device_id_type=MESH).wait_recv()
 
-    def same_core(s):
-        return lax.rem(chip + s, chips) * 2 + core
-
-    def other_core(s):
-        return lax.rem(chip + s, chips) * 2 + 1 - core
-
-    @pl.loop(0, CHUNKS)
-    def _(c):
-        local_x(c).start()
-        local_c(c).start()
+    def each_part(step, first=0):
+        @pl.loop(first, z.main)
+        def _(c):
+            step(full(c))
+        for part in z.tail:
+            step(part)
 
     local_r = pltpu.make_async_copy(rw_hbm, rw_v, w_local.at[0])
     local_r.start()
     local_l = pltpu.make_async_copy(lw_hbm, lw_v, w_local.at[1])
     local_l.start()
+
     local_r.wait()
     local_l.wait()
     shape = (z.mp * z.pad, z.bs)
@@ -133,22 +163,33 @@
     rg[me] = rwt[p]
     lg[d] = lwt[...]
 
-    pl.semaphore_wait(barrier, z.n - 1)
-
-    def send_x(c):
+    pl.semaphore_wait(barrier, near)
+
+    def send_x(part):
         for s in range(1, chips):
-            send_own(c, s, same_core(s)).start()
-        send_own(c, 0, partner).start()
-
-    send_x(0)
-
-    @pl.loop(1, z.n)
-    def _(s):
-        o = lax.rem(me + s, z.n)
-        q = lax.rem(o, z.mp)
-        pltpu.make_async_remote_copy(
-            src_ref=rwt.at[q], dst_ref=rg.at[me], send_sem=rw_send, recv_sem=rw_recv,
-            device_id=(o // z.mp, q), device_id_type=MESH).start()
+            send_own(part, s, same_core(s)).start()
+        send_own(part, 0, partner).start()
+
+    for s in range(1, z.mp):
+        q = lax.rem(p + s, z.mp)
+        pltpu.make_async_remote_copy(
+            src_ref=rwt.at[q], dst_ref=rg.at[me], send_sem=ra_send, recv_sem=ra_recv,
+            device_id=(d, q), device_id_type=MESH).start()
+
+    each_part(send_x)
+
+    if z.cube:
+        for r in range(z.rounds):
+            pl.semaphore_signal(met.at[r], inc=1, device_id=(across(d, r), p), device_id_type=MESH)
+            pl.semaphore_wait(met.at[r], 1)
+
+    @each_part
+    def _(part):
+        local_x(part).start()
+        local_c(part).start()
+
+    def count(ref, sem):
+        pltpu.make_async_copy(ref, ref, sem).wait()
 
     @pl.loop(1, z.dp)
     def _(s):
@@ -156,9 +197,14 @@
             src_ref=lwt, dst_ref=lg.at[d], send_sem=lw_send, recv_sem=lw_recv,
             device_id=(lax.rem(d + s, z.dp), p), device_id_type=MESH).start()
 
-    @pl.loop(1, CHUNKS)
-    def _(c):
-        send_x(c)
+    count(rg.at[pl.ds(0, z.mp - 1)], ra_recv)
+    mine = rg.at[pl.ds(d * z.mp, z.mp)]
+
+    @pl.loop(1, z.dp)
+    def _(s):
+        pltpu.make_async_remote_copy(
+            src_ref=mine, dst_ref=mine, send_sem=rw_send, recv_sem=rw_recv,
+            device_id=(lax.rem(d + s, z.dp), p), device_id_type=MESH).start()
 
     for dd in range(z.dp):
         shape = (z.orow, z.feat)
@@ -176,9 +222,6 @@
     gracc[...] = jnp.zeros_like(gracc)
     glacc[...] = jnp.zeros_like(glacc)
 
-    def count(ref, sem):
-        pltpu.make_async_copy(ref, ref, sem).wait()
-
     count(lg.at[pl.ds(0, z.dp - 1)], lw_recv)
     left = None
     for dd in range(z.dp):
@@ -192,7 +235,7 @@
         keep = iota((z.fj, z.rh), 0) // z.bs == iota((z.fj, z.rh), 1) % z.jl
         lt[jg] = jnp.where(keep, piece, 0.0).astype(BF)
 
-    count(rg.at[pl.ds(0, z.n - 1)], rw_recv)
+    count(rg.at[pl.ds(0, z.n - z.mp)], rw_recv)
     right = None
     for dd in range(z.dp):
         part = dot_nn(rg[dd * z.mp:(dd + 1) * z.mp].reshape(z.mp * z.pad, z.orow), p1[dd])
@@ -210,17 +253,17 @@
             keep = (iota(shape, 0) // z.jl) % z.own == iota(shape, 1) // z.bs
             wt[g, :, s * z.feat:(s + 1) * z.feat] = jnp.where(keep, piece, 0.0).astype(BF)
 
-    @pl.loop(0, CHUNKS)
-    def _(c):
-        local_x(c).wait()
-        local_c(c).wait()
+    @each_part
+    def _(part):
+        local_x(part).wait()
+        local_c(part).wait()
         for s in range(1, chips):
-            arrived(c, same_core(s))
-            forward(c, chips + s, same_core(s)).start()
-        arrived(c, partner)
+            arrived(part, same_core(s))
+            forward(part, chips + s, same_core(s)).start()
+        arrived(part, partner)
         for s in range(1, chips):
-            arrived(c, other_core(s))
-        r = rows(c)
+            arrived(part, other_core(s))
+        r = pl.ds(part[1], part[2])
         xs = [join([xfull[g * z.gs + s, r] for s in range(z.gs)]) for g in range(z.groups)]
         inner = [dot_nt(xs[g], wt[g]).astype(BF) for g in range(z.groups)]
         back = []
@@ -282,14 +325,15 @@
     lrecv[d] = lsend[d]
     rrecv[me] = rsend[me]
 
-    @pl.loop(0, CHUNKS)
-    def _(c):
+    @each_part
+    def _(part):
         for s in range(1, chips):
-            send_own(c, s, same_core(s)).wait_send()
-            forward(c, chips + s, same_core(s)).wait_send()
-        send_own(c, 0, partner).wait_send()
-
-    count(rg.at[pl.ds(0, z.n - 1)], rw_send)
+            send_own(part, s, same_core(s)).wait_send()
+            forward(part, chips + s, same_core(s)).wait_send()
+        send_own(part, 0, partner).wait_send()
+
+    count(rg.at[pl.ds(0, z.mp - 1)], ra_send)
+    count(rg.at[pl.ds(0, z.n - z.mp)], rw_send)
     count(lg.at[pl.ds(0, z.dp - 1)], lw_send)
 
     count(lrecv.at[pl.ds(0, z.dp - 1)], gl_recv)
@@ -306,6 +350,15 @@
     count(rsend.at[pl.ds(0, z.n - 1)], gr_send)
 
 
+def store(*refs):
+    sems = refs[6]
+    copies = [pltpu.make_async_copy(refs[k], refs[k + 3], sems.at[k]) for k in range(3)]
+    for copy in copies:
+        copy.start()
+    for copy in copies:
+        copy.wait()
+
+
 def shards(z, tokens, right_weight, left_weight, cotangent):
     rw = right_weight.reshape(z.orow, z.bs)
     lw = left_weight.reshape(z.orow, z.bs)
@@ -316,8 +369,8 @@
         functools.partial(kernel, z),
         out_shape=(
             pltpu.VMEM((z.tok, z.feat), BF),
-            jax.ShapeDtypeStruct((z.orow, z.bs) if z.direct else (z.mp, z.pad, z.orow), F32),
-            jax.ShapeDtypeStruct((z.orow, z.bs) if z.direct else (z.bs, z.orow), F32),
+            pltpu.VMEM((z.orow, z.bs) if z.direct else (z.mp, z.pad, z.orow), F32),
+            pltpu.VMEM((z.orow, z.bs) if z.direct else (z.bs, z.orow), F32),
         ),
         in_specs=[hbm] * 4,
         out_specs=(vmem, vmem, vmem),
@@ -340,16 +393,25 @@
             pltpu.VMEM((z.n, z.pad, z.orow), BF),
             pltpu.VMEM((z.dp, z.bs, z.orow), BF),
             pltpu.VMEM((z.dp, z.bs, z.orow), BF),
-            dma((z.mp, CHUNKS)),
-            dma((z.mp, CHUNKS)),
-            dma((CHUNKS,)),
-            dma((CHUNKS,)),
+            dma((z.mp, z.parts)),
+            dma((z.mp, z.parts)),
+            dma((z.parts,)),
+            dma((z.parts,)),
             dma((2,)),
-            dma, dma, dma, dma, dma, dma, dma, dma,
+            dma, dma, dma, dma, dma, dma, dma, dma, dma, dma,
+            pltpu.SemaphoreType.REGULAR((max(1, z.rounds),)),
         ],
         compiler_params=pltpu.CompilerParams(
             collective_id=0, has_side_effects=True, vmem_limit_bytes=61 * 1024 * 1024),
     )(tokens, cotangent, rw, lw)
+    act, gr, gl = pl.pallas_call(
+        store,
+        out_shape=[jax.ShapeDtypeStruct(v.shape, v.dtype) for v in (act, gr, gl)],
+        in_specs=[vmem] * 3,
+        out_specs=[hbm] * 3,
+        scratch_shapes=[dma((3,))],
+        compiler_params=pltpu.CompilerParams(vmem_limit_bytes=1024 * 1024),
+    )(act, gr, gl)
     if z.direct:
         return act, gr.reshape(z.own, z.rows, z.bs), gl.reshape(z.own, z.rows, z.bs)
     gr = gr[:, :z.own].reshape(z.mp * z.own, z.own, z.rows).transpose(1, 2, 0)

time: 72.4 us -> 67.3 us (0.930)
  local copies, waits for them, and re-layouts: 2.59 us -> 0 us
  Pallas kernels: 68.6 us -> 66.1 us
    pallas_call x1, Pallas kernels: 68.6 us -> 64.7 us  [shards(): pl.pallas_call(functools.partial(kernel, z), out_shape=(pltpu.VMEM((z.tok...]
    unnamed x7 -> x0, local copies, waits for them, and re-layouts: 2.59 us -> none
    pallas_call x0 -> x1, Pallas kernels: none -> 1.37 us  [shards(): pl.pallas_call(store, out_shape=[jax.ShapeDtypeStruct(v.shape, v.dtype) f...]
where the time goes in v1:
time: 67.3 us; the launch traced here: 66.7 us
  Pallas kernels  66.1 us (98%)
    pallas_call x1, Pallas kernels, shards(): pl.pallas_call(functools.partial(kernel, z), out_shape=(pltpu.VMEM((z.tok...  64.7 us
    pallas_call x1, Pallas kernels, shards(): pl.pallas_call(store, out_shape=[jax.ShapeDtypeStruct(v.shape, v.dtype) f...  1.37 us

profile of v1, /device:TPU:1, one launch (start us, length us, event | category | flops | bytes accessed | tf_op | source)
XLA Modules:
  0.0 66.7 jit_solution(16149744474740621303)
XLA Ops:
  0.6 64.7 %shard_map.67 = (bf16[1024,1024]{1,0:T(8,128)(2,1)S(1)}, f32[128,64]{1,0:T(8,128)S(1)}, f32[128,64]{1,0:T(8,128)S(1)}) custom-call(bf16[1024,1024]{1,0:T(8,128)(2,1)} %x_hbm.1, bf16[1024,1024]{1,0:T(8,128)(2,1)} %cot_hbm.1, bf16[128,64]{1,0:T(8,128)(2,1)} %bitcast.4, bf16[128,64]{1,0:T(8,128)(2,1)} %bitcast.5), custom_call_target="tpu_custom_call" | custom-call | tf_op jit(solution)/shard_map/pallas_call | solution.py:368
  65.3 1.4 %shard_map.68 = (bf16[1024,1024]{1,0:T(8,128)(2,1)}, f32[128,64]{1,0:T(8,128)}, f32[128,64]{1,0:T(8,128)}) custom-call(bf16[1024,1024]{1,0:T(8,128)(2,1)S(1)} %get-tuple-element.9.refs_0_, f32[128,64]{1,0:T(8,128)S(1)} %get-tuple-element.10.refs_1_, f32[128,64]{1,0:T(8,128)S(1)} %get-tuple-element.11.refs_2_), custom_call_target="tpu_custom_call" | custom-call | tf_op jit(solution)/shard_map/pallas_call | solution.py:407

commit v2 on v1

--- a/solution.py
+++ b/solution.py
@@ -72,6 +72,9 @@
             self.tail.append((self.main + len(self.tail), start, self.tc // part))
             start += self.tc // part
         self.parts = self.main + len(self.tail)
+        self.n1 = CHUNKS // 2
+        self.n2 = CHUNKS - self.n1
+        self.split = self.direct and self.gs == 1 and self.jl == 8 and 128 % width == 0 and self.own % (256 // width) == 0
         self.rounds = n_dp.bit_length() - 1
         self.cube = n_dp == 1 << self.rounds
 
@@ -350,6 +353,440 @@
     count(rsend.at[pl.ds(0, z.n - 1)], gr_send)
 
 
+def split_kernel(z, x_hbm, cot_hbm, rw_hbm, lw_hbm, act, gr_ref, gl_ref,
+                 xfull, x2, cot, rw_v, lw_v, rwt, lwt, rg, rg2, lg, p1, p2, wt, wt2, lt, gracc, glacc,
+                 isend, irecv, dsend, drecv, fsend, frecv, rsend, rrecv, lsend, lrecv,
+                 x_recv, x_send, x_local, c_local, w_local, i_send, i_recv, d_send, d_recv,
+                 f_send, f_recv, gr_send, gr_recv,
+                 rw_send, rw_recv, lw_send, lw_recv, gl_send, gl_recv, ra_send, ra_recv, rb_send, rb_recv, met):
+    d, p = lax.axis_index("dp"), lax.axis_index("mp")
+    me = d * z.mp + p
+    core = lax.rem(p, 2)
+    partner = p + 1 - 2 * core
+    chip = p // 2
+    chips = z.mp // 2
+    n1, n2, tc = z.n1, z.n2, z.tc
+    first = n1 * tc
+
+    def same_core(s):
+        return lax.rem(chip + s, chips) * 2 + core
+
+    def other_core(s):
+        return lax.rem(chip + s, chips) * 2 + 1 - core
+
+    barrier = pltpu.get_barrier_semaphore()
+    if z.cube:
+        for s in range(1, z.mp):
+            pl.semaphore_signal(barrier, inc=1, device_id=(d, lax.rem(p + s, z.mp)), device_id_type=MESH)
+        for r in range(z.rounds):
+            pl.semaphore_signal(barrier, inc=1, device_id=(across(d, r), p), device_id_type=MESH)
+        near = z.mp - 1 + z.rounds
+    else:
+        @pl.loop(1, z.n)
+        def _(s):
+            o = lax.rem(me + s, z.n)
+            pl.semaphore_signal(barrier, inc=1, device_id=(o // z.mp, lax.rem(o, z.mp)), device_id_type=MESH)
+        near = z.n - 1
+
+    def rows(c):
+        return pl.ds(pl.multiple_of(c * tc, tc), tc)
+
+    def later(c):
+        return pl.ds(pl.multiple_of(first + c * tc, tc), tc)
+
+    def local_x(c):
+        return pltpu.make_async_copy(x_hbm.at[rows(c)], xfull.at[p, rows(c)], x_local.at[c])
+
+    def local_x2(c):
+        return pltpu.make_async_copy(x_hbm.at[later(c)], x2.at[rows(c)], x_local.at[n1 + c])
+
+    def local_c(c):
+        return pltpu.make_async_copy(cot_hbm.at[rows(c)], cot.at[rows(c)], c_local.at[c])
+
+    def send_own(c, kind, target):
+        return pltpu.make_async_remote_copy(
+            src_ref=x_hbm.at[rows(c)], dst_ref=xfull.at[p, rows(c)],
+            send_sem=x_send.at[kind, c], recv_sem=x_recv.at[p, c],
+            device_id=(d, target), device_id_type=MESH)
+
+    def forward(c, kind, source):
+        return pltpu.make_async_remote_copy(
+            src_ref=xfull.at[source, rows(c)], dst_ref=xfull.at[source, rows(c)],
+            send_sem=x_send.at[kind, c], recv_sem=x_recv.at[source, c],
+            device_id=(d, partner), device_id_type=MESH)
+
+    def arrived(c, source):
+        forward(c, 0, source).wait_recv()
+
+    def each_mp(send):
+        for s in range(1, chips):
+            send(same_core(s))
+            send(other_core(s))
+        send(partner)
+
+    def send_inner(c, q):
+        pltpu.make_async_remote_copy(
+            src_ref=isend.at[q, rows(c)], dst_ref=irecv.at[p, rows(c)],
+            send_sem=i_send.at[c], recv_sem=i_recv.at[c],
+            device_id=(d, q), device_id_type=MESH).start()
+
+    def send_dinner(c, jg, q):
+        pltpu.make_async_remote_copy(
+            src_ref=dsend.at[jg, q, rows(c)], dst_ref=drecv.at[jg, p, rows(c)],
+            send_sem=d_send.at[jg, c], recv_sem=d_recv.at[jg, c],
+            device_id=(d, q), device_id_type=MESH).start()
+
+    def send_first(q):
+        pltpu.make_async_remote_copy(
+            src_ref=fsend.at[q], dst_ref=frecv.at[p], send_sem=f_send, recv_sem=f_recv,
+            device_id=(d, q), device_id_type=MESH).start()
+
+    def count(ref, sem):
+        pltpu.make_async_copy(ref, ref, sem).wait()
+
+    def others(ref):
+        return ref.at[pl.ds(0, z.mp - 1)]
+
+    local_r = pltpu.make_async_copy(rw_hbm, rw_v, w_local.at[0])
+    local_r.start()
+    local_l = pltpu.make_async_copy(lw_hbm, lw_v, w_local.at[1])
+    local_l.start()
+    local_r.wait()
+    local_l.wait()
+    shape = (z.mp * z.pad, z.bs)
+    a, b = iota(shape, 0), iota(shape, 1)
+    wide = ones_where((a % z.pad < z.own) & (b == (a // z.pad) * z.own + a % z.pad))
+    rwt[...] = dot_nt(wide, rw_v[...]).astype(BF).reshape(z.mp, z.pad, z.orow)
+    shape = (z.bs, z.bs)
+    lwt[...] = dot_nt(ones_where(iota(shape, 0) == iota(shape, 1)), lw_v[...]).astype(BF)
+    rg[me] = rwt[p]
+    rg2[d] = rwt[...]
+    lg[d] = lwt[...]
+    pl.semaphore_wait(barrier, near)
+
+    for s in range(1, z.mp):
+        q = lax.rem(p + s, z.mp)
+        pltpu.make_async_remote_copy(
+            src_ref=rwt.at[q], dst_ref=rg.at[me], send_sem=ra_send, recv_sem=ra_recv,
+            device_id=(d, q), device_id_type=MESH).start()
+
+    @pl.loop(0, n1)
+    def _(c):
+        for s in range(1, chips):
+            send_own(c, s, same_core(s)).start()
+        send_own(c, 0, partner).start()
+
+    if z.cube:
+        for r in range(z.rounds):
+            pl.semaphore_signal(met.at[r], inc=1, device_id=(across(d, r), p), device_id_type=MESH)
+            pl.semaphore_wait(met.at[r], 1)
+
+    @pl.loop(0, n1)
+    def _(c):
+        local_x(c).start()
+        local_c(c).start()
+
+    @pl.loop(0, n2)
+    def _(c):
+        local_x2(c).start()
+        local_c(n1 + c).start()
+
+    @pl.loop(1, z.dp)
+    def _(s):
+        pltpu.make_async_remote_copy(
+            src_ref=lwt, dst_ref=lg.at[d], send_sem=lw_send, recv_sem=lw_recv,
+            device_id=(lax.rem(d + s, z.dp), p), device_id_type=MESH).start()
+
+    count(others(rg), ra_recv)
+    mine = rg.at[pl.ds(d * z.mp, z.mp)]
+
+    @pl.loop(1, z.dp)
+    def _(s):
+        pltpu.make_async_remote_copy(
+            src_ref=mine, dst_ref=mine, send_sem=rw_send, recv_sem=rw_recv,
+            device_id=(lax.rem(d + s, z.dp), p), device_id_type=MESH).start()
+
+    @pl.loop(1, z.dp)
+    def _(s):
+        pltpu.make_async_remote_copy(
+            src_ref=rwt, dst_ref=rg2.at[d], send_sem=rb_send, recv_sem=rb_recv,
+            device_id=(lax.rem(d + s, z.dp), p), device_id_type=MESH).start()
+
+    for dd in range(z.dp):
+        shape = (z.orow, z.feat)
+        a, b = iota(shape, 0), iota(shape, 1)
+        source = (b // z.bs) * z.rows + (b % z.bs) - dd * z.rows
+        inside = (b % z.bs) // z.rows == dd
+        p1[dd] = ones_where(inside & (a == source))
+        shape = (z.orow, z.blocks * z.own)
+        a, b = iota(shape, 0), iota(shape, 1)
+        jg = b // z.rh
+        i_all = (b % z.rh) // z.jl
+        j = jg * z.jl + b % z.jl
+        inside = i_all // z.rows == dd
+        p2[dd] = ones_where(inside & (a == j * z.rows + i_all % z.rows))
+    gracc[...] = jnp.zeros_like(gracc)
+    glacc[...] = jnp.zeros_like(glacc)
+
+    count(lg.at[pl.ds(0, z.dp - 1)], lw_recv)
+    left = None
+    for dd in range(z.dp):
+        part = dot_nn(lg[dd], p2[dd])
+        left = part if left is None else left + part
+    left = left.astype(BF)
+    shape = (z.fj, z.bs)
+    spread = ones_where(iota(shape, 0) % z.bs == iota(shape, 1))
+    for jg in range(z.jg):
+        piece = dot_nn(spread, left[:, jg * z.rh:(jg + 1) * z.rh])
+        keep = iota((z.fj, z.rh), 0) // z.bs == iota((z.fj, z.rh), 1) % z.jl
+        lt[jg] = jnp.where(keep, piece, 0.0).astype(BF)
+
+    def expand(blocks, target):
+        right = None
+        for dd in range(z.dp):
+            part = dot_nn(blocks(dd).reshape(z.mp * z.pad, z.orow), p1[dd])
+            right = part if right is None else right + part
+        right = right.astype(BF)
+        for g in range(z.mp):
+            shape = (z.ng, z.mp * z.pad)
+            a, b = iota(shape, 0), iota(shape, 1)
+            pick = ones_where(b == g * z.pad + (a // z.nj) * z.jl + a % z.jl)
+            piece = dot_nn(pick, right)
+            shape = (z.ng, z.feat)
+            keep = (iota(shape, 0) // z.jl) % z.own == iota(shape, 1) // z.bs
+            target[g] = jnp.where(keep, piece, 0.0).astype(BF)
+
+    count(rg.at[pl.ds(0, z.n - z.mp)], rw_recv)
+    expand(lambda dd: rg[dd * z.mp:(dd + 1) * z.mp], wt)
+    count(rg2.at[pl.ds(0, z.dp - 1)], rb_recv)
+    expand(lambda dd: rg2[dd], wt2)
+
+    def layer(inner, r):
+        back = []
+        for jg in range(z.jg):
+            mixed = join([v[:, jg * z.nj:(jg + 1) * z.nj] for v in inner])
+            pre = dot_nt(mixed, lt[jg])
+            cdf = 0.5 * (1.0 + lax.erf(pre * 0.7071067811865476))
+            slope = cdf + pre * (jnp.exp(-0.5 * pre * pre) * 0.3989422804014327)
+            cols = pl.ds(jg * z.fj, z.fj)
+            act[r, cols] = (pre * cdf).astype(BF)
+            dpre = (cot[r, cols].astype(F32) * slope).astype(BF)
+            glacc[jg] += dot_tn(dpre, mixed)
+            back.append(dot_nn(dpre, lt[jg]).astype(BF))
+        return back
+
+    @pl.loop(0, n1)
+    def _(c):
+        local_x(c).wait()
+        local_c(c).wait()
+        for s in range(1, chips):
+            arrived(c, same_core(s))
+            forward(c, chips + s, same_core(s)).start()
+        arrived(c, partner)
+        for s in range(1, chips):
+            arrived(c, other_core(s))
+        r = rows(c)
+        xs = [xfull[g, r] for g in range(z.mp)]
+        back = layer([dot_nt(xs[g], wt[g]).astype(BF) for g in range(z.mp)], r)
+        for g in range(z.mp):
+            dinner = join([v[:, g * z.nj:(g + 1) * z.nj] for v in back])
+            gracc[g] += dot_tn(dinner, xs[g])
+
+        @pl.loop(c * n2 // n1, (c + 1) * n2 // n1)
+        def _(e):
+            local_x2(e).wait()
+            own = x2[rows(e)]
+            for q in range(z.mp):
+                isend[q, rows(e)] = dot_nt(own, wt2[q]).astype(BF)
+            each_mp(functools.partial(send_inner, e))
+            irecv[p, rows(e)] = isend[p, rows(e)]
+
+    per = 128 // z.bs
+    lane = iota((z.jl, 128), 1) // z.bs
+
+    def diagonal(tile):
+        parts = []
+        for v in range(z.own // per):
+            piece = tile(v * per, v)
+            for w in range(1, per):
+                piece = jnp.where(lane == w, tile(v * per + w, v), piece)
+            parts.append(piece)
+        return join(parts)
+
+    for g in range(z.mp):
+        halves = []
+        for jg in range(z.jg):
+            halves.append(diagonal(lambda i, v: gracc[
+                g, jg * z.nj + i * z.jl:jg * z.nj + (i + 1) * z.jl, v * 128:(v + 1) * 128]))
+        fsend[g] = join(halves, axis=0).astype(BF)
+    each_mp(send_first)
+    frecv[p] = fsend[p]
+
+    @pl.loop(0, n2)
+    def _(c):
+        local_c(n1 + c).wait()
+        r = rows(c)
+        count(irecv.at[pl.ds(0, z.mp - 1), r], i_recv.at[c])
+        back = layer([irecv[g, r] for g in range(z.mp)], later(c))
+        for jg in range(z.jg):
+            for g in range(z.mp):
+                dsend[jg, g, r] = back[jg][:, g * z.nj:(g + 1) * z.nj]
+            drecv[jg, p, r] = dsend[jg, p, r]
+        each_mp(functools.partial(send_dinner, c, 0))
+
+    for jg in range(1, z.jg):
+        @pl.loop(0, n2)
+        def _(c):
+            each_mp(functools.partial(send_dinner, c, jg))
+
+    shape = (z.bs, z.fj)
+    fold = ones_where(iota(shape, 1) % z.bs == iota(shape, 0))
+    lefts = []
+    for jg in range(z.jg):
+        keep = iota((z.fj, z.rh), 0) // z.bs == iota((z.fj, z.rh), 1) % z.jl
+        lefts.append(dot_nn(fold, jnp.where(keep, glacc[jg], 0.0).astype(BF)).astype(BF))
+    left = join(lefts)
+    for dd in range(z.dp):
+        lsend[dd] = dot_nt(left, p2[dd]).astype(BF)
+
+    @pl.loop(1, z.dp)
+    def _(s):
+        o = lax.rem(d + s, z.dp)
+        pltpu.make_async_remote_copy(
+            src_ref=lsend.at[o], dst_ref=lrecv.at[d], send_sem=gl_send, recv_sem=gl_recv,
+            device_id=(o, p), device_id_type=MESH).start()
+    lrecv[d] = lsend[d]
+
+    quad = 256 // z.bs
+
+    def piece_of(jg, lo, hi):
+        turned = [drecv[jg, q, lo * tc:hi * tc].T for q in range(z.mp)]
+        parts = []
+        for a in range(z.own // quad):
+            m = quad * z.jl
+            lhs = join([t[a * m:(a + 1) * m] for t in turned], axis=0)
+            full = dot_nn(lhs, x2[lo * tc:hi * tc, a * 256:(a + 1) * 256])
+            blocks = []
+            for q in range(z.mp):
+                tiles = []
+                for v in range(quad // per):
+                    base = q * m + v * per * z.jl
+                    piece = full[base:base + z.jl, v * 128:(v + 1) * 128]
+                    for w in range(1, per):
+                        base += z.jl
+                        piece = jnp.where(lane == w, full[base:base + z.jl, v * 128:(v + 1) * 128], piece)
+                    tiles.append(piece)
+                blocks.append(join(tiles))
+            parts.append(join(blocks, axis=0))
+        return join(parts)
+
+    count(others(frecv), f_recv)
+    early = frecv[...].astype(F32)
+    for jg in range(z.jg):
+        total = join([early[q, jg * z.jl:(jg + 1) * z.jl] for q in range(z.mp)], axis=0)
+        cuts = (0, n2) if jg < z.jg - 1 or n2 < 2 else (0, n2 - 1, n2)
+        for lo, hi in zip(cuts[:-1], cuts[1:]):
+            for c in range(lo, hi):
+                count(drecv.at[jg, pl.ds(0, z.mp - 1), pl.ds(c * tc, tc)], d_recv.at[jg, c])
+            total = total + piece_of(jg, lo, hi)
+        total = total.astype(BF)
+        for dd in range(z.dp):
+            rsend[jg, dd] = dot_nt(total, p1[dd]).astype(BF)
+
+        @pl.loop(1, z.dp)
+        def _(s):
+            o = lax.rem(d + s, z.dp)
+            pltpu.make_async_remote_copy(
+                src_ref=rsend.at[jg, o], dst_ref=rrecv.at[jg, d],
+                send_sem=gr_send.at[jg], recv_sem=gr_recv.at[jg],
+                device_id=(o, p), device_id_type=MESH).start()
+        rrecv[jg, d] = rsend[jg, d]
+
+    @pl.loop(0, n1)
+    def _(c):
+        for s in range(1, chips):
+            send_own(c, s, same_core(s)).wait_send()
+            forward(c, chips + s, same_core(s)).wait_send()
+        send_own(c, 0, partner).wait_send()
+
+    @pl.loop(0, n2)
+    def _(c):
+        count(isend.at[pl.ds(0, z.mp - 1), rows(c)], i_send.at[c])
+        for jg in range(z.jg):
+            count(dsend.at[jg, pl.ds(0, z.mp - 1), rows(c)], d_send.at[jg, c])
+
+    count(others(rg), ra_send)
+    count(others(fsend), f_send)
+    count(rg.at[pl.ds(0, z.n - z.mp)], rw_send)
+    count(rg2.at[pl.ds(0, z.dp - 1)], rb_send)
+    count(lg.at[pl.ds(0, z.dp - 1)], lw_send)
+
+    count(lrecv.at[pl.ds(0, z.dp - 1)], gl_recv)
+    total = lrecv[0].astype(F32)
+    for dd in range(1, z.dp):
+        total = total + lrecv[dd].astype(F32)
+    gl_ref[...] = total.T
+    totals = []
+    for jg in range(z.jg):
+        count(rrecv.at[jg, pl.ds(0, z.dp - 1)], gr_recv.at[jg])
+        total = rrecv[jg, 0].astype(F32)
+        for dd in range(1, z.dp):
+            total = total + rrecv[jg, dd].astype(F32)
+        totals.append(total)
+    total = join([t[q * z.jl:(q + 1) * z.jl] for q in range(z.mp) for t in totals], axis=0)
+    gr_ref[...] = total.T
+    count(lsend.at[pl.ds(0, z.dp - 1)], gl_send)
+    for jg in range(z.jg):
+        count(rsend.at[jg, pl.ds(0, z.dp - 1)], gr_send.at[jg])
+
+
+def split_scratch(z):
+    dma = pltpu.SemaphoreType.DMA
+    return [
+        pltpu.VMEM((z.mp, z.n1 * z.tc, z.feat), BF),
+        pltpu.VMEM((z.n2 * z.tc, z.feat), BF),
+        pltpu.VMEM((z.tok, z.feat), BF),
+        pltpu.VMEM((z.orow, z.bs), BF),
+        pltpu.VMEM((z.orow, z.bs), BF),
+        pltpu.VMEM((z.mp, z.pad, z.orow), BF),
+        pltpu.VMEM((z.bs, z.orow), BF),
+        pltpu.VMEM((z.n, z.pad, z.orow), BF),
+        pltpu.VMEM((z.dp, z.mp, z.pad, z.orow), BF),
+        pltpu.VMEM((z.dp, z.bs, z.orow), BF),
+        pltpu.VMEM((z.dp, z.orow, z.feat), BF),
+        pltpu.VMEM((z.dp, z.orow, z.blocks * z.own), BF),
+        pltpu.VMEM((z.mp, z.ng, z.feat), BF),
+        pltpu.VMEM((z.mp, z.ng, z.feat), BF),
+        pltpu.VMEM((z.jg, z.fj, z.rh), BF),
+        pltpu.VMEM((z.mp, z.ng, z.feat), F32),
+        pltpu.VMEM((z.jg, z.fj, z.rh), F32),
+        pltpu.VMEM((z.mp, z.n2 * z.tc, z.ng), BF),
+        pltpu.VMEM((z.mp, z.n2 * z.tc, z.ng), BF),
+        pltpu.VMEM((z.jg, z.mp, z.n2 * z.tc, z.nj), BF),
+        pltpu.VMEM((z.jg, z.mp, z.n2 * z.tc, z.nj), BF),
+        pltpu.VMEM((z.mp, z.own, z.feat), BF),
+        pltpu.VMEM((z.mp, z.own, z.feat), BF),
+        pltpu.VMEM((z.jg, z.dp, z.mp * z.jl, z.orow), BF),
+        pltpu.VMEM((z.jg, z.dp, z.mp * z.jl, z.orow), BF),
+        pltpu.VMEM((z.dp, z.bs, z.orow), BF),
+        pltpu.VMEM((z.dp, z.bs, z.orow), BF),
+        dma((z.mp, z.n1)),
+        dma((z.mp, z.n1)),
+        dma((CHUNKS,)),
+        dma((CHUNKS,)),
+        dma((2,)),
+        dma((z.n2,)),
+        dma((z.n2,)),
+        dma((z.jg, z.n2)),
+        dma((z.jg, z.n2)),
+        dma, dma,
+        dma((z.jg,)),
+        dma((z.jg,)),
+        dma, dma, dma, dma, dma, dma, dma, dma, dma, dma,
+        pltpu.SemaphoreType.REGULAR((max(1, z.rounds),)),
+    ]
+
+
 def store(*refs):
     sems = refs[6]
     copies = [pltpu.make_async_copy(refs[k], refs[k + 3], sems.at[k]) for k in range(3)]
@@ -366,7 +803,7 @@
     vmem = pl.BlockSpec(memory_space=pltpu.VMEM)
     dma = pltpu.SemaphoreType.DMA
     act, gr, gl = pl.pallas_call(
-        functools.partial(kernel, z),
+        functools.partial(split_kernel if z.split else kernel, z),
         out_shape=(
             pltpu.VMEM((z.tok, z.feat), BF),
             pltpu.VMEM((z.orow, z.bs) if z.direct else (z.mp, z.pad, z.orow), F32),
@@ -374,7 +811,7 @@
         ),
         in_specs=[hbm] * 4,
         out_specs=(vmem, vmem, vmem),
-        scratch_shapes=[
+        scratch_shapes=split_scratch(z) if z.split else [
             pltpu.VMEM((z.mp, z.tok, z.feat), BF),
             pltpu.VMEM((z.tok, z.feat), BF),
             pltpu.VMEM((z.orow, z.bs), BF),

time: 67.3 us -> 63.8 us (0.948)
  Pallas kernels: 66.1 us -> 62 us
    pallas_call x1, Pallas kernels: 64.7 us -> 60.6 us  [shards(): pl.pallas_call(functools.partial(split_kernel if z.split else kernel, z),...]
where the time goes in v2:
time: 63.8 us; the launch traced here: 62.6 us
  Pallas kernels  62 us (97%)
  between operations  0.64 us (1%)
    pallas_call x1, Pallas kernels, shards(): pl.pallas_call(functools.partial(split_kernel if z.split else kernel, z),...  60.6 us
    pallas_call x1, Pallas kernels, shards(): pl.pallas_call(store, out_shape=[jax.ShapeDtypeStruct(v.shape, v.dtype) f...  1.37 us

profile of v2, /device:TPU:1, one launch (start us, length us, event | category | flops | bytes accessed | tf_op | source)
XLA Modules:
  0.0 62.6 jit_solution(6241064387897599270)
XLA Ops:
  0.6 60.6 %shard_map.67 = (bf16[1024,1024]{1,0:T(8,128)(2,1)S(1)}, f32[128,64]{1,0:T(8,128)S(1)}, f32[128,64]{1,0:T(8,128)S(1)}) custom-call(bf16[1024,1024]{1,0:T(8,128)(2,1)} %x_hbm.1, bf16[1024,1024]{1,0:T(8,128)(2,1)} %cot_hbm.1, bf16[128,64]{1,0:T(8,128)(2,1)} %bitcast.4, bf16[128,64]{1,0:T(8,128)(2,1)} %bitcast.5), custom_call_target="tpu_custom_call" | custom-call | tf_op jit(solution)/shard_map/pallas_call | solution.py:805
  61.2 1.4 %shard_map.68 = (bf16[1024,1024]{1,0:T(8,128)(2,1)}, f32[128,64]{1,0:T(8,128)}, f32[128,64]{1,0:T(8,128)}) custom-call(bf16[1024,1024]{1,0:T(8,128)(2,1)S(1)} %get-tuple-element.9.refs_0_, f32[128,64]{1,0:T(8,128)S(1)} %get-tuple-element.10.refs_1_, f32[128,64]{1,0:T(8,128)S(1)} %get-tuple-element.11.refs_2_), custom_call_target="tpu_custom_call" | custom-call | tf_op jit(solution)/shard_map/pallas_call | solution.py:844

commit v3 on v2

--- a/solution.py
+++ b/solution.py
@@ -74,7 +74,13 @@
         self.parts = self.main + len(self.tail)
         self.n1 = CHUNKS // 2
         self.n2 = CHUNKS - self.n1
-        self.split = self.direct and self.gs == 1 and self.jl == 8 and 128 % width == 0 and self.own % (256 // width) == 0
+        self.early = min(2, self.n1)
+        self.quad = 256 // width
+        self.quads = self.own // max(1, self.quad)
+        self.unit = self.quad * self.rows
+        self.slots = 128 // self.unit
+        self.units = self.jg * (n_mp // 2)
+        self.split = self.gs == 1 and self.jl == 8 and self.rows == 8 and self.orow == 128 and width == 64 and n_mp == 4
         self.rounds = n_dp.bit_length() - 1
         self.cube = n_dp == 1 << self.rounds
 
@@ -355,9 +361,9 @@
 
 def split_kernel(z, x_hbm, cot_hbm, rw_hbm, lw_hbm, act, gr_ref, gl_ref,
                  xfull, x2, cot, rw_v, lw_v, rwt, lwt, rg, rg2, lg, p1, p2, wt, wt2, lt, gracc, glacc,
-                 isend, irecv, dsend, drecv, fsend, frecv, rsend, rrecv, lsend, lrecv,
+                 isend, irecv, dsend, drecv, turn, esend, erecv, fsend, frecv, rsend, rrecv, final, lsend, lrecv,
                  x_recv, x_send, x_local, c_local, w_local, i_send, i_recv, d_send, d_recv,
-                 f_send, f_recv, gr_send, gr_recv,
+                 e_send, e_recv, f_send, f_recv, gr_send, gr_recv,
                  rw_send, rw_recv, lw_send, lw_recv, gl_send, gl_recv, ra_send, ra_recv, rb_send, rb_recv, met):
     d, p = lax.axis_index("dp"), lax.axis_index("mp")
     me = d * z.mp + p
@@ -405,7 +411,7 @@
 
     def send_own(c, kind, target):
         return pltpu.make_async_remote_copy(
-            src_ref=x_hbm.at[rows(c)], dst_ref=xfull.at[p, rows(c)],
+            src_ref=xfull.at[p, rows(c)], dst_ref=xfull.at[p, rows(c)],
             send_sem=x_send.at[kind, c], recv_sem=x_recv.at[p, c],
             device_id=(d, target), device_id_type=MESH)
 
@@ -424,16 +430,22 @@
             send(other_core(s))
         send(partner)
 
+    def dinners(c, jg):
+        for s in range(1, chips):
+            send_dinner(c, jg, 1, same_core(s))
+            send_dinner(c, jg, 1, other_core(s))
+        send_dinner(c, jg, 0, partner)
+
     def send_inner(c, q):
         pltpu.make_async_remote_copy(
             src_ref=isend.at[q, rows(c)], dst_ref=irecv.at[p, rows(c)],
             send_sem=i_send.at[c], recv_sem=i_recv.at[c],
             device_id=(d, q), device_id_type=MESH).start()
 
-    def send_dinner(c, jg, q):
+    def send_dinner(c, jg, kind, q):
         pltpu.make_async_remote_copy(
             src_ref=dsend.at[jg, q, rows(c)], dst_ref=drecv.at[jg, p, rows(c)],
-            send_sem=d_send.at[jg, c], recv_sem=d_recv.at[jg, c],
+            send_sem=d_send.at[jg, c], recv_sem=d_recv.at[jg, kind, c],
             device_id=(d, q), device_id_type=MESH).start()
 
     def send_first(q):
@@ -446,11 +458,24 @@
 
     def others(ref):
         return ref.at[pl.ds(0, z.mp - 1)]
+
+    @pl.loop(0, n1)
+    def _(c):
+        local_x(c).start()
 
     local_r = pltpu.make_async_copy(rw_hbm, rw_v, w_local.at[0])
     local_r.start()
     local_l = pltpu.make_async_copy(lw_hbm, lw_v, w_local.at[1])
     local_l.start()
+
+    def send_x(c):
+        local_x(c).wait()
+        for s in range(1, chips):
+            send_own(c, s, same_core(s)).start()
+        send_own(c, 0, partner).start()
+
+    pl.semaphore_wait(barrier, near)
+    send_x(0)
     local_r.wait()
     local_l.wait()
     shape = (z.mp * z.pad, z.bs)
@@ -462,19 +487,15 @@
     rg[me] = rwt[p]
     rg2[d] = rwt[...]
     lg[d] = lwt[...]
-    pl.semaphore_wait(barrier, near)
-
     for s in range(1, z.mp):
         q = lax.rem(p + s, z.mp)
         pltpu.make_async_remote_copy(
             src_ref=rwt.at[q], dst_ref=rg.at[me], send_sem=ra_send, recv_sem=ra_recv,
             device_id=(d, q), device_id_type=MESH).start()
 
-    @pl.loop(0, n1)
+    @pl.loop(1, n1)
     def _(c):
-        for s in range(1, chips):
-            send_own(c, s, same_core(s)).start()
-        send_own(c, 0, partner).start()
+        send_x(c)
 
     if z.cube:
         for r in range(z.rounds):
@@ -483,7 +504,6 @@
 
     @pl.loop(0, n1)
     def _(c):
-        local_x(c).start()
         local_c(c).start()
 
     @pl.loop(0, n2)
@@ -494,6 +514,12 @@
     @pl.loop(1, z.dp)
     def _(s):
         pltpu.make_async_remote_copy(
+            src_ref=rwt, dst_ref=rg2.at[d], send_sem=rb_send, recv_sem=rb_recv,
+            device_id=(lax.rem(d + s, z.dp), p), device_id_type=MESH).start()
+
+    @pl.loop(1, z.dp)
+    def _(s):
+        pltpu.make_async_remote_copy(
             src_ref=lwt, dst_ref=lg.at[d], send_sem=lw_send, recv_sem=lw_recv,
             device_id=(lax.rem(d + s, z.dp), p), device_id_type=MESH).start()
 
@@ -504,12 +530,6 @@
     def _(s):
         pltpu.make_async_remote_copy(
             src_ref=mine, dst_ref=mine, send_sem=rw_send, recv_sem=rw_recv,
-            device_id=(lax.rem(d + s, z.dp), p), device_id_type=MESH).start()
-
-    @pl.loop(1, z.dp)
-    def _(s):
-        pltpu.make_async_remote_copy(
-            src_ref=rwt, dst_ref=rg2.at[d], send_sem=rb_send, recv_sem=rb_recv,
             device_id=(lax.rem(d + s, z.dp), p), device_id_type=MESH).start()
 
     for dd in range(z.dp):
@@ -525,21 +545,15 @@
         j = jg * z.jl + b % z.jl
         inside = i_all // z.rows == dd
         p2[dd] = ones_where(inside & (a == j * z.rows + i_all % z.rows))
+    for a in range(z.quads):
+        shape = (256, 256)
+        u, v = iota(shape, 0), iota(shape, 1)
+        owner = (u % z.bs) // z.rows
+        slot = (v % 128) // z.unit
+        same = (u // z.bs == (v % z.unit) // z.rows) & (u % z.rows == v % z.rows)
+        turn[a] = ones_where(same & (owner // z.slots == v // 128) & ((owner + a) % z.slots == slot))
     gracc[...] = jnp.zeros_like(gracc)
     glacc[...] = jnp.zeros_like(glacc)
-
-    count(lg.at[pl.ds(0, z.dp - 1)], lw_recv)
-    left = None
-    for dd in range(z.dp):
-        part = dot_nn(lg[dd], p2[dd])
-        left = part if left is None else left + part
-    left = left.astype(BF)
-    shape = (z.fj, z.bs)
-    spread = ones_where(iota(shape, 0) % z.bs == iota(shape, 1))
-    for jg in range(z.jg):
-        piece = dot_nn(spread, left[:, jg * z.rh:(jg + 1) * z.rh])
-        keep = iota((z.fj, z.rh), 0) // z.bs == iota((z.fj, z.rh), 1) % z.jl
-        lt[jg] = jnp.where(keep, piece, 0.0).astype(BF)
 
     def expand(blocks, target):
         right = None
@@ -556,10 +570,44 @@
             keep = (iota(shape, 0) // z.jl) % z.own == iota(shape, 1) // z.bs
             target[g] = jnp.where(keep, piece, 0.0).astype(BF)
 
+    count(rg2.at[pl.ds(0, z.dp - 1)], rb_recv)
+    expand(lambda dd: rg2[dd], wt2)
+
+    @pl.loop(0, n2)
+    def _(c):
+        local_x2(c).wait()
+        own = x2[rows(c)]
+        for q in range(z.mp):
+            isend[q, rows(c)] = dot_nt(own, wt2[q]).astype(BF)
+        each_mp(functools.partial(send_inner, c))
+        irecv[p, rows(c)] = isend[p, rows(c)]
+        for a in range(z.quads):
+            cols = slice(a * 256, (a + 1) * 256)
+            x2[rows(c), cols] = dot_nn(own[:, cols], turn[a]).astype(BF)
+
+    def pass_on(c):
+        for s in range(1, chips):
+            arrived(c, same_core(s))
+            forward(c, chips + s, same_core(s)).start()
+
+    for c in range(z.early):
+        pass_on(c)
+
+    count(lg.at[pl.ds(0, z.dp - 1)], lw_recv)
+    left = None
+    for dd in range(z.dp):
+        part = dot_nn(lg[dd], p2[dd])
+        left = part if left is None else left + part
+    left = left.astype(BF)
+    shape = (z.fj, z.bs)
+    spread = ones_where(iota(shape, 0) % z.bs == iota(shape, 1))
+    for jg in range(z.jg):
+        piece = dot_nn(spread, left[:, jg * z.rh:(jg + 1) * z.rh])
+        keep = iota((z.fj, z.rh), 0) // z.bs == iota((z.fj, z.rh), 1) % z.jl
+        lt[jg] = jnp.where(keep, piece, 0.0).astype(BF)
+
     count(rg.at[pl.ds(0, z.n - z.mp)], rw_recv)
     expand(lambda dd: rg[dd * z.mp:(dd + 1) * z.mp], wt)
-    count(rg2.at[pl.ds(0, z.dp - 1)], rb_recv)
-    expand(lambda dd: rg2[dd], wt2)
 
     def layer(inner, r):
         back = []
@@ -577,11 +625,11 @@
 
     @pl.loop(0, n1)
     def _(c):
-        local_x(c).wait()
         local_c(c).wait()
-        for s in range(1, chips):
-            arrived(c, same_core(s))
-            forward(c, chips + s, same_core(s)).start()
+        @pl.when(c >= z.early)
+        def _():
+            pass_on(c)
+
         arrived(c, partner)
         for s in range(1, chips):
             arrived(c, other_core(s))
@@ -592,15 +640,6 @@
             dinner = join([v[:, g * z.nj:(g + 1) * z.nj] for v in back])
             gracc[g] += dot_tn(dinner, xs[g])
 
-        @pl.loop(c * n2 // n1, (c + 1) * n2 // n1)
-        def _(e):
-            local_x2(e).wait()
-            own = x2[rows(e)]
-            for q in range(z.mp):
-                isend[q, rows(e)] = dot_nt(own, wt2[q]).astype(BF)
-            each_mp(functools.partial(send_inner, e))
-            irecv[p, rows(e)] = isend[p, rows(e)]
-
     per = 128 // z.bs
     lane = iota((z.jl, 128), 1) // z.bs
 
@@ -613,14 +652,22 @@
             parts.append(piece)
         return join(parts)
 
+    pieces = []
     for g in range(z.mp):
-        halves = []
         for jg in range(z.jg):
-            halves.append(diagonal(lambda i, v: gracc[
+            pieces.append(diagonal(lambda i, v: gracc[
                 g, jg * z.nj + i * z.jl:jg * z.nj + (i + 1) * z.jl, v * 128:(v + 1) * 128]))
-        fsend[g] = join(halves, axis=0).astype(BF)
-    each_mp(send_first)
-    frecv[p] = fsend[p]
+    pieces = join(pieces, axis=0).astype(BF)
+    for dd in range(z.dp):
+        esend[dd] = dot_nt(pieces, p1[dd]).astype(BF)
+
+    @pl.loop(1, z.dp)
+    def _(s):
+        o = lax.rem(d + s, z.dp)
+        pltpu.make_async_remote_copy(
+            src_ref=esend.at[o], dst_ref=erecv.at[d], send_sem=e_send, recv_sem=e_recv,
+            device_id=(o, p), device_id_type=MESH).start()
+    erecv[d] = esend[d]
 
     @pl.loop(0, n2)
     def _(c):
@@ -632,12 +679,12 @@
             for g in range(z.mp):
                 dsend[jg, g, r] = back[jg][:, g * z.nj:(g + 1) * z.nj]
             drecv[jg, p, r] = dsend[jg, p, r]
-        each_mp(functools.partial(send_dinner, c, 0))
+        dinners(c, 0)
 
     for jg in range(1, z.jg):
         @pl.loop(0, n2)
         def _(c):
-            each_mp(functools.partial(send_dinner, c, jg))
+            dinners(c, jg)
 
     shape = (z.bs, z.fj)
     fold = ones_where(iota(shape, 1) % z.bs == iota(shape, 0))
@@ -657,50 +704,73 @@
             device_id=(o, p), device_id_type=MESH).start()
     lrecv[d] = lsend[d]
 
-    quad = 256 // z.bs
-
-    def piece_of(jg, lo, hi):
-        turned = [drecv[jg, q, lo * tc:hi * tc].T for q in range(z.mp)]
-        parts = []
-        for a in range(z.own // quad):
-            m = quad * z.jl
+    count(erecv.at[pl.ds(0, z.dp - 1)], e_recv)
+    total = erecv[0].astype(F32)
+    for dd in range(1, z.dp):
+        total = total + erecv[dd].astype(F32)
+    fsend[...] = total.astype(BF).reshape(z.mp, z.own, z.orow)
+    each_mp(send_first)
+    frecv[p] = fsend[p]
+
+    shape = (z.jl, 128)
+    block_of = (iota(shape, 1) % z.unit) // z.rows
+    slot_of = iota(shape, 1) // z.unit
+
+    def pick(options, which):
+        out = options[0]
+        for w in range(1, len(options)):
+            out = jnp.where(which == w, options[w], out)
+        return out
+
+    def owned(jg, s, lo, hi):
+        base = lax.rem(chip + s, chips) * 2
+        turned = [drecv[jg, base + k, lo * tc:hi * tc].T for k in range(2)]
+        m = z.quad * z.jl
+        tiles = []
+        for a in range(z.quads):
             lhs = join([t[a * m:(a + 1) * m] for t in turned], axis=0)
             full = dot_nn(lhs, x2[lo * tc:hi * tc, a * 256:(a + 1) * 256])
-            blocks = []
-            for q in range(z.mp):
-                tiles = []
-                for v in range(quad // per):
-                    base = q * m + v * per * z.jl
-                    piece = full[base:base + z.jl, v * 128:(v + 1) * 128]
-                    for w in range(1, per):
-                        base += z.jl
-                        piece = jnp.where(lane == w, full[base:base + z.jl, v * 128:(v + 1) * 128], piece)
-                    tiles.append(piece)
-                blocks.append(join(tiles))
-            parts.append(join(blocks, axis=0))
-        return join(parts)
-
-    count(others(frecv), f_recv)
-    early = frecv[...].astype(F32)
-    for jg in range(z.jg):
-        total = join([early[q, jg * z.jl:(jg + 1) * z.jl] for q in range(z.mp)], axis=0)
-        cuts = (0, n2) if jg < z.jg - 1 or n2 < 2 else (0, n2 - 1, n2)
-        for lo, hi in zip(cuts[:-1], cuts[1:]):
-            for c in range(lo, hi):
-                count(drecv.at[jg, pl.ds(0, z.mp - 1), pl.ds(c * tc, tc)], d_recv.at[jg, c])
-            total = total + piece_of(jg, lo, hi)
-        total = total.astype(BF)
+            tiles.append([[pick([full[k * m + w * z.jl:k * m + (w + 1) * z.jl, h * 128:(h + 1) * 128]
+                                 for w in range(z.quad)], block_of) for k in range(2)] for h in range(256 // 128)])
+        out = []
         for dd in range(z.dp):
-            rsend[jg, dd] = dot_nt(total, p1[dd]).astype(BF)
+            h, t = dd // z.slots, dd % z.slots
+            out.append(join([pick([tiles[(w - t) % z.slots][h][k] for w in range(z.slots)], slot_of)
+                             for k in range(2)], axis=0))
+        return out
+
+    def exchange(unit, blocks):
+        for dd in range(z.dp):
+            rsend[unit, dd] = blocks[dd].astype(BF)
 
         @pl.loop(1, z.dp)
         def _(s):
             o = lax.rem(d + s, z.dp)
             pltpu.make_async_remote_copy(
-                src_ref=rsend.at[jg, o], dst_ref=rrecv.at[jg, d],
-                send_sem=gr_send.at[jg], recv_sem=gr_recv.at[jg],
+                src_ref=rsend.at[unit, o], dst_ref=rrecv.at[unit, d],
+                send_sem=gr_send.at[unit], recv_sem=gr_recv.at[unit],
                 device_id=(o, p), device_id_type=MESH).start()
-        rrecv[jg, d] = rsend[jg, d]
+        rrecv[unit, d] = rsend[unit, d]
+
+    def landed(jg, kind, lo, hi):
+        for c in range(lo, hi):
+            amount = z.mp - 2 if kind else 1
+            count(drecv.at[jg, pl.ds(0, amount), pl.ds(c * tc, tc)], d_recv.at[jg, kind, c])
+
+    units = [(jg, s) for s in range(chips) for jg in range(z.jg)]
+    for s in range(chips):
+        for jg in range(z.jg):
+            unit = units.index((jg, s))
+            if s == 1 and jg == z.jg - 1 and n2 > 1:
+                landed(jg, 1, 0, n2 - 1)
+                early = owned(jg, s, 0, n2 - 1)
+                landed(jg, 1, n2 - 1, n2)
+                late = owned(jg, s, n2 - 1, n2)
+                exchange(unit, [u + v for u, v in zip(early, late)])
+            else:
+                if s < 2:
+                    landed(jg, s, 0, n2)
+                exchange(unit, owned(jg, s, 0, n2))
 
     @pl.loop(0, n1)
     def _(c):
@@ -716,6 +786,7 @@
             count(dsend.at[jg, pl.ds(0, z.mp - 1), rows(c)], d_send.at[jg, c])
 
     count(others(rg), ra_send)
+    count(esend.at[pl.ds(0, z.dp - 1)], e_send)
     count(others(fsend), f_send)
     count(rg.at[pl.ds(0, z.n - z.mp)], rw_send)
     count(rg2.at[pl.ds(0, z.dp - 1)], rb_send)
@@ -726,18 +797,21 @@
     for dd in range(1, z.dp):
         total = total + lrecv[dd].astype(F32)
     gl_ref[...] = total.T
-    totals = []
-    for jg in range(z.jg):
-        count(rrecv.at[jg, pl.ds(0, z.dp - 1)], gr_recv.at[jg])
-        total = rrecv[jg, 0].astype(F32)
+    count(others(frecv), f_recv)
+    spin = lax.rem(128 - lax.rem(d, z.slots) * z.unit, 128)
+    for unit, (jg, s) in enumerate(units):
+        count(rrecv.at[unit, pl.ds(0, z.dp - 1)], gr_recv.at[unit])
+        total = rrecv[unit, 0].astype(F32)
         for dd in range(1, z.dp):
-            total = total + rrecv[jg, dd].astype(F32)
-        totals.append(total)
-    total = join([t[q * z.jl:(q + 1) * z.jl] for q in range(z.mp) for t in totals], axis=0)
+            total = total + rrecv[unit, dd].astype(F32)
+        total = pltpu.roll(total, spin, 1)
+        for k in range(2):
+            final[lax.rem(chip + s, chips) * 2 + k, jg] = total[k * z.jl:(k + 1) * z.jl]
+    total = final[...].reshape(z.blocks, z.orow) + frecv[...].astype(F32).reshape(z.blocks, z.orow)
     gr_ref[...] = total.T
     count(lsend.at[pl.ds(0, z.dp - 1)], gl_send)
-    for jg in range(z.jg):
-        count(rsend.at[jg, pl.ds(0, z.dp - 1)], gr_send.at[jg])
+    for unit in range(len(units)):
+        count(rsend.at[unit, pl.ds(0, z.dp - 1)], gr_send.at[unit])
 
 
 def split_scratch(z):
@@ -764,10 +838,14 @@
         pltpu.VMEM((z.mp, z.n2 * z.tc, z.ng), BF),
         pltpu.VMEM((z.jg, z.mp, z.n2 * z.tc, z.nj), BF),
         pltpu.VMEM((z.jg, z.mp, z.n2 * z.tc, z.nj), BF),
-        pltpu.VMEM((z.mp, z.own, z.feat), BF),
-        pltpu.VMEM((z.mp, z.own, z.feat), BF),
-        pltpu.VMEM((z.jg, z.dp, z.mp * z.jl, z.orow), BF),
-        pltpu.VMEM((z.jg, z.dp, z.mp * z.jl, z.orow), BF),
+        pltpu.VMEM((z.quads, 256, 256), BF),
+        pltpu.VMEM((z.dp, z.blocks, z.orow), BF),
+        pltpu.VMEM((z.dp, z.blocks, z.orow), BF),
+        pltpu.VMEM((z.mp, z.own, z.orow), BF),
+        pltpu.VMEM((z.mp, z.own, z.orow), BF),
+        pltpu.VMEM((z.units, z.dp, 2 * z.jl, z.orow), BF),
+        pltpu.VMEM((z.units, z.dp, 2 * z.jl, z.orow), BF),
+        pltpu.VMEM((z.mp, z.jg, z.jl, z.orow), F32),
         pltpu.VMEM((z.dp, z.bs, z.orow), BF),
         pltpu.VMEM((z.dp, z.bs, z.orow), BF),
         dma((z.mp, z.n1)),
@@ -778,18 +856,21 @@
         dma((z.n2,)),
         dma((z.n2,)),
         dma((z.jg, z.n2)),
-        dma((z.jg, z.n2)),
-        dma, dma,
-        dma((z.jg,)),
-        dma((z.jg,)),
+        dma((z.jg, 2, z.n2)),
+        dma, dma, dma, dma,
+        dma((z.units,)),
+        dma((z.units,)),
         dma, dma, dma, dma, dma, dma, dma, dma, dma, dma,
         pltpu.SemaphoreType.REGULAR((max(1, z.rounds),)),
     ]
 
 
-def store(*refs):
-    sems = refs[6]
-    copies = [pltpu.make_async_copy(refs[k], refs[k + 3], sems.at[k]) for k in range(3)]
+def store(act, gr, gl, act_out, gr_out, gl_out, sems):
+    size = act.shape[0] // CHUNKS
+    copies = [pltpu.make_async_copy(gr, gr_out, sems.at[0]), pltpu.make_async_copy(gl, gl_out, sems.at[1])]
+    for c in range(CHUNKS):
+        r = pl.ds(c * size, size)
+        copies.append(pltpu.make_async_copy(act.at[r], act_out.at[r], sems.at[2 + c]))
     for copy in copies:
         copy.start()
     for copy in copies:
@@ -846,7 +927,7 @@
         out_shape=[jax.ShapeDtypeStruct(v.shape, v.dtype) for v in (act, gr, gl)],
         in_specs=[vmem] * 3,
         out_specs=[hbm] * 3,
-        scratch_shapes=[dma((3,))],
+        scratch_shapes=[dma((2 + CHUNKS,))],
         compiler_params=pltpu.CompilerParams(vmem_limit_bytes=1024 * 1024),
     )(act, gr, gl)
     if z.direct:

time: 63.8 us -> 59.5 us (0.933)
  the two profiles are of different devices: /device:TPU:1 before, /device:TPU:0 now
where the time goes in v3:
time: 59.5 us; the launch traced here: 59.4 us
  Pallas kernels  58.7 us (99%)
  between operations  0.64 us (1%)
    pallas_call x1, Pallas kernels, shards(): pl.pallas_call(functools.partial(split_kernel if z.split else kernel, z),...  57.3 us
    pallas_call x1, Pallas kernels, shards(): pl.pallas_call(store, out_shape=[jax.ShapeDtypeStruct(v.shape, v.dtype) f...  1.44 us

profile of v3, /device:TPU:0, one launch (start us, length us, event | category | flops | bytes accessed | tf_op | source)
XLA Modules:
  0.0 59.4 jit_solution(15593762831608829086)
XLA Ops:
  0.6 57.3 %shard_map.67 = (bf16[1024,1024]{1,0:T(8,128)(2,1)S(1)}, f32[128,64]{1,0:T(8,128)S(1)}, f32[128,64]{1,0:T(8,128)S(1)}) custom-call(bf16[1024,1024]{1,0:T(8,128)(2,1)} %x_hbm.1, bf16[1024,1024]{1,0:T(8,128)(2,1)} %cot_hbm.1, bf16[128,64]{1,0:T(8,128)(2,1)} %bitcast.4, bf16[128,64]{1,0:T(8,128)(2,1)} %bitcast.5), custom_call_target="tpu_custom_call" | custom-call | tf_op jit(solution)/shard_map/pallas_call | solution.py:886
  57.9 1.4 %shard_map.68 = (bf16[1024,1024]{1,0:T(8,128)(2,1)}, f32[128,64]{1,0:T(8,128)}, f32[128,64]{1,0:T(8,128)}) custom-call(bf16[1024,1024]{1,0:T(8,128)(2,1)S(1)} %get-tuple-element.9.act, f32[128,64]{1,0:T(8,128)S(1)} %get-tuple-element.10.gr, f32[128,64]{1,0:T(8,128)S(1)} %get-tuple-element.11.gl), custom_call_target="tpu_custom_call" | custom-call | tf_op jit(solution)/shard_map/pallas_call | solution.py:925
